TPU v7x, 128 devices: a whole 4x4x4 slice. The times are simulated.
128 devices in a mesh: row: 4 (over z), col: 16 (over x, y_hi, core), depth: 2 (over y_lo).
Axes of the slice: x: 4, y: 4 (y_hi: 2, y_lo: 2; y = y_hi * 2 + y_lo), z: 4, core: 2. Of those that a mesh axis runs over, the one named last changes fastest.
Arguments:
- tokens: bfloat16 [8192, 8192], P(('row', 'col'), 'depth'), may hold values from -0.15625 to 0.15625
- weight: bfloat16 [8192, 8192], P('depth', ('col', 'row')), may hold values from -0.0625 to 0.0625
- grad_output: bfloat16 [8192, 8192], P('row', ('col', 'depth')), may hold values from -6 to 6
Outputs:
- grad_input: bfloat16 [8192, 8192], P(('row', 'col'), 'depth')
- grad_weight: bfloat16 [8192, 8192], P('depth', ('col', 'row'))
All inputs are finite; a program needn't handle non-finite values.
Results may differ from a plain program's by a relative error of at most 0.001.
Values may be sent and summed in bfloat16 or wider, within the bound.
A program may use at most 128 MiB of HBM per device.

v0:
```python
import jax
import jax.numpy as jnp
from jax import lax
from jax.sharding import PartitionSpec as P

last_with_last = (((1,), (1,)), ((), ()))
first_with_first = (((0,), (0,)), ((), ()))


def split_up(value, dim, devices):
    before, after = (value.shape[:dim], value.shape[dim + 1 :])
    return jnp.moveaxis(value.reshape(*before, devices, -1, *after), dim, 0)


def sum_at_owner(value, axis, dim):
    devices = lax.axis_size(axis)
    blocks = lax.all_to_all(split_up(value, dim, devices), axis, 0, 0, tiled=True)
    return jnp.sum(blocks, axis=0)


def copy_for_each(value, axis):
    copies = jnp.broadcast_to(value, (lax.axis_size(axis), *value.shape))
    return lax.all_to_all(copies, axis, split_axis=0, concat_axis=0, tiled=True)


def joined_along(blocks, dim):
    lengths = list(blocks.shape[1:])
    lengths[dim] *= blocks.shape[0]
    return jnp.moveaxis(blocks, 0, dim).reshape(lengths)


def gather_directly(value, axis, dim):
    blocks = copy_for_each(value, axis)
    return joined_along(blocks, dim)


def input_grads(weight, grad_block):
    weight_block = lax.all_gather(weight, "row", axis=1, tiled=True)
    summed = lax.psum_scatter(
        lax.dot_general(
            grad_block, weight_block, last_with_last, preferred_element_type=jnp.float32
        ),
        "col",
        scatter_dimension=0,
        tiled=True,
    )
    return summed.astype(jnp.bfloat16)


def weight_grads(tokens, grad_block):
    partial_value = lax.dot_general(
        lax.all_gather(tokens, "col", axis=0, tiled=True),
        grad_block,
        first_with_first,
        preferred_element_type=jnp.float32,
    )
    return sum_at_owner(partial_value, "row", 1).astype(jnp.bfloat16)


def per_device(tokens, weight, grad_output):
    grad_block = gather_directly(grad_output, "depth", 1)
    grad_input = input_grads(weight, grad_block)
    grad_weight = weight_grads(tokens, grad_block)
    return (grad_input, grad_weight)


def solution(mesh):
    return jax.shard_map(
        per_device,
        mesh=mesh,
        in_specs=(
            P(("row", "col"), "depth"),
            P("depth", ("col", "row")),
            P("row", ("col", "depth")),
        ),
        out_specs=(P(("row", "col"), "depth"), P("depth", ("col", "row"))),
        check_vma=False,
    )
```

profile of v0, /device:TPU:1, one launch (start us, length us, event | category | flops | bytes accessed | tf_op | source)
XLA Modules:
  0.0 447.5 jit_solution(4611471758320542201)
XLA Ops:
  7.2 0.0 copy-start
  7.2 0.0 all-gather.3.cloned.1.call-start
  7.2 0.7 all-gather.3.cloned.1.call-update
  7.9 0.0 all-gather.5.cloned.1.call-start
  8.0 2.3 copy.6
  10.2 0.0 all-gather.5.cloned.1.call-update
  10.2 0.0 reduce-scatter.2.cloned.1.call-start
  10.3 0.0 copy-done
  10.3 0.6 copy.5
  11.0 0.2 broadcast_in_dim.3
  11.2 27.3 %all_to_all.10 = bf16[2,2048,256]{1,2,0:T(8,128)(2,1)S(1)} all-to-all(bf16[2,2048,256]{1,2,0:T(8,128)(2,1)S(1)} %broadcast_in_dim.3), channel_id=1, replica_groups=mesh['row'=4,'col'=16,'depth'=2] {'depth'}, dimensions={0} | all-to-all | bytes 4194304 | tf_op jit(solution)/shard_map/all_to_all | solution.py:23
  38.5 24.6 %all-gather.3.cloned.1.call-done = bf16[4096,512]{1,0:T(8,128)(2,1)} async-done(((bf16[4096,128]{1,0:T(8,128)(2,1)}), bf16[4096,512]{1,0:T(8,128)(2,1)}) %all-gather.3.cloned.1.call-update) | async-done | bytes 4194320 | tf_op jit(solution)/shard_map/all_gather | solution.py:38
  63.1 18.4 %fusion.5 = f32[2048,4096]{1,0:T(8,128)} fusion(bf16[2048,512]{0,1:T(8,128)(2,1)S(1)} %bitcast.17, bf16[4096,512]{1,0:T(8,128)(2,1)} %all-gather.3.cloned.1.call-done), kind=kOutput, calls=%fused_computation.3 | convolution fusion | flops 8589934592 | bytes 39845888 | tf_op jit(solution)/shard_map/dot_general | solution.py:40
  81.5 0.0 reduce-scatter.2.cloned.1.call-update
  81.5 109.2 %all-gather.5.cloned.1.call-done = bf16[2048,4096]{0,1:T(8,128)(2,1)} async-done(((bf16[128,4096]{0,1:T(8,128)(2,1)}), bf16[2048,4096]{0,1:T(8,128)(2,1)}) %all-gather.5.cloned.1.call-update) | async-done | bytes 16777232 | tf_op jit(solution)/shard_map/all_gather | solution.py:52
  190.7 12.3 %fusion.2 = f32[4,4096,128]{2,1,0:T(8,128)S(1)} fusion(bf16[4,128,2048]{2,1,0:T(8,128)(2,1)S(1)} %bitcast.18, bf16[2048,4096]{0,1:T(8,128)(2,1)} %all-gather.5.cloned.1.call-done), kind=kOutput, calls=%fused_computation.2 | convolution fusion | flops 8589934592 | bytes 27262976 | tf_op jit(solution)/shard_map/dot_general | solution.py:51
  202.9 97.3 %all_to_all.11 = f32[4,4096,128]{2,1,0:T(8,128)} all-to-all(f32[4,4096,128]{2,1,0:T(8,128)S(1)} %fusion.2), channel_id=1, replica_groups=mesh['row'=4,'col'=16,'depth'=2] {'row'}, dimensions={0} | all-to-all | bytes 16777216 | tf_op jit(solution)/shard_map/all_to_all | solution.py:17
  300.3 5.2 %reduce_sum.9 = bf16[4096,128]{1,0:T(8,128)(2,1)} reduce(f32[4,4096,128]{2,1,0:T(8,128)} %all_to_all.11, f32[]{:T(128)} %constant.0.clone.1), dimensions={0}, to_apply=%region_1.0 | reduce | flops 1572864 | bytes 9437188 | tf_op jit(solution)/shard_map/reduce_sum | solution.py:18
  305.5 132.7 %reduce-scatter.2.cloned.1.call-done = f32[128,4096]{1,0:T(8,128)} async-done(((f32[2048,4096]{1,0:T(8,128)}), f32[128,4096]{1,0:T(8,128)}) %reduce-scatter.2.cloned.1.call-update) | async-done | bytes 2097168 | tf_op jit(solution)/shard_map/reduce_scatter | solution.py:39
  438.2 2.7 convert_element_type.6
Async XLA Ops:
  7.2 3.1 copy-start
  7.2 55.9 %all-gather.3.cloned.1.call-start = ((), (), s32[]{:S(2)}) async-start(), calls=%async_computation.3 | async-start | bytes 5242880 | tf_op jit(solution)/shard_map/all_gather | solution.py:38
  7.9 182.8 %all-gather.5.cloned.1.call-start = ((), (), s32[]{:S(2)}) async-start(), calls=%async_computation.5 | async-start | bytes 17825792 | tf_op jit(solution)/shard_map/all_gather | solution.py:52
  10.2 428.0 %reduce-scatter.2.cloned.1.call-start = ((), (), s32[]{:S(2)}) async-start(), calls=%async_computation.4 | async-start | bytes 35651584 | tf_op jit(solution)/shard_map/reduce_scatter | solution.py:39
Sparse Core Ops, SparseCore 0:
  9.6 53.4 all-gather.2
  65.9 124.6 all-gather.4
  195.1 243.0 reduce-scatter.1
where the time goes:
time: 450 us; the launch traced here: 447 us
  waiting for transfers between devices  267 us (59%)
  blocking collectives  125 us (28%)
  matrix products  30.6 us (7%)
  between operations  13.8 us (3%)
  other arithmetic  7.92 us (2%)
    reduce_scatter x1, waiting for transfers between devices, input_grads(): lax.psum_scatter(lax.dot_general(grad_block, weight_block, last_with_last...  133 us
    all_gather x1, waiting for transfers between devices, weight_grads(): lax.all_gather(tokens, 'col', axis=0, tiled=True)  109 us
    all_to_all x1, blocking collectives, sum_at_owner(): lax.all_to_all(split_up(value, dim, devices), axis, 0, 0, tiled=True)  97.3 us
    all_to_all x1, blocking collectives, copy_for_each(): return lax.all_to_all(copies, axis, split_axis=0, concat_axis=0, tiled=True)  27.3 us
    all_gather x1, waiting for transfers between devices, input_grads(): weight_block = lax.all_gather(weight, 'row', axis=1, tiled=True)  24.6 us
    dot_general x1, matrix products, input_grads(): lax.dot_general(grad_block, weight_block, last_with_last, preferred_eleme...  18.4 us
    dot_general x1, matrix products, weight_grads(): lax.dot_general(lax.all_gather(tokens, 'col', axis=0, tiled=True), grad_b...  12.3 us
  transfers between devices with their start and end apart: 3, of which 3 were waited for; matrix products, arithmetic and copies ran while one was open for 9% of the time, Pallas kernels for 0%

commit v1 on v0

v1 whole, which is shorter than its diff:
```python
import jax
import jax.numpy as jnp
from jax import lax
from jax.experimental import pallas as pl
from jax.experimental.pallas import tpu as pltpu
from jax.sharding import PartitionSpec as P

MESH = pl.DeviceIdType.MESH
BF16, F32 = jnp.bfloat16, jnp.float32

B = 512
TILE = 256
CODE_ROWS = B + 16
TOP = 320.0
POWER = 15


def encode(tile, ref):
    top = jnp.max(jnp.abs(tile), axis=0, keepdims=True)
    scale = (top * 1.01 + 1e-30).astype(BF16)
    u = tile * (TOP / scale.astype(F32))
    u3 = u * u * u
    u6 = u3 * u3
    ref[0:B, :] = (u6 * u6 * u3).astype(BF16)
    ref[B:CODE_ROWS, :] = jnp.broadcast_to(scale.astype(F32), (16, TILE)).astype(BF16)


def decode(ref):
    code = ref[0:B, :].astype(F32)
    scale = ref[B:CODE_ROWS, :].astype(F32)[0:1] * (1.0 / TOP)
    size = jnp.exp2(jnp.log2(jnp.abs(code)) * (1.0 / POWER))
    return jnp.where(code < 0, -size, size) * scale


def kernel(
    t_hbm, w_hbm, g_hbm, gi_out, gw_out,
    t_loc, tt_loc, tt, w, g, gi_tx, gi_hop, gi_rx, gw_tx, gw_hop, gw_rx, gi_fin, gw_fin,
    local_sem, g_local_sem,
    w_ex_send, t_ex_send, w_ag_send, t_ag_send, w_fw_send, t_fw_send, w_recv, t_recv,
    g_ring_send, g_fw_send, g_mate_send, g_recv, g_mate_recv,
    gi_send, gi_hop_recv, gi_recv, gw_send, gw_hop_recv, gw_recv,
    gi_fin_send, gi_fin_recv, gw_fin_send, gw_fin_recv,
):
    z, col, yl = lax.axis_index("row"), lax.axis_index("col"), lax.axis_index("depth")
    x, q = col // 4, col % 4
    yh, core = q // 2, q % 2
    y = 2 * yh + yl

    def at_x(k):
        return (z, ((x + k) % 4) * 4 + q, yl)

    def at_z(k):
        return ((z + k) % 4, col, yl)

    def at_y(k):
        other = (y + k) % 4
        return (z, x * 4 + (other // 2) * 2 + core, other % 2)

    mate = (z, x * 4 + yh * 2 + (1 - core), yl)

    def partner(k):
        return (z, x * 4 + k, 1 - yl)

    def send(src, dst, send_sem, recv_sem, to):
        copy = pltpu.make_async_remote_copy(
            src_ref=src, dst_ref=dst, send_sem=send_sem, recv_sem=recv_sem, device_id=to, device_id_type=MESH
        )
        copy.start()
        return copy

    def arrived(ref, sem):
        pltpu.make_async_remote_copy(
            src_ref=ref, dst_ref=ref, send_sem=sem, recv_sem=sem, device_id=mate, device_id_type=MESH
        ).wait_recv()

    sent = []

    def lanes(block, k):
        return pl.ds(pl.multiple_of(block * B + k * 128, 128), 128)

    t_copy = pltpu.make_async_copy(t_hbm, t_loc, local_sem)
    t_copy.start()
    g_copies = []
    for e in range(2):
        g_copies.append(
            pltpu.make_async_copy(g_hbm.at[:, pl.ds(e * 128, 128)], g.at[:, lanes(2 * yl + e, q)], g_local_sem.at[e])
        )
        g_copies[-1].start()

    barrier = pltpu.get_barrier_semaphore()
    peers = [at_x(1), at_x(3), at_z(1), at_z(3), mate] + [partner(k) for k in range(4)]
    for peer in peers:
        pl.semaphore_signal(barrier, inc=1, device_id=peer, device_id_type=MESH)
    pl.semaphore_wait(barrier, len(peers))

    for k in range(4):
        sent.append(
            send(w_hbm.at[pl.ds(k * 1024, 1024), :], w.at[:, lanes(z, q)], w_ex_send.at[k], w_recv.at[0, q], partner(k))
        )
    t_copy.wait()
    for k in range(4):
        for part in range(2):
            at = k * 1024 + part * 512
            tt_loc[at : at + 512, :] = t_loc[:, at : at + 512].T
        sent.append(
            send(tt_loc.at[pl.ds(k * 1024, 1024), :], tt.at[:, lanes(x, q)], t_ex_send.at[k], t_recv.at[0, q], partner(k))
        )

    order = (2, 1, 3, 0)

    def g_piece(r, dy, other_core, e):
        owner = (y + dy) % 4
        rows = pl.ds(pl.multiple_of(((x + order[r]) % 4) * B, B), B)
        k = (owner // 2) * 2 + (core if not other_core else 1 - core)
        return g.at[rows, lanes(2 * (owner % 2) + e, k)]

    def g_own(r):
        for e in range(2):
            piece = g_piece(r, 0, False, e)
            sent.append(send(piece, piece, g_ring_send.at[r, 0, e], g_recv.at[r, 0, e], at_y(1)))
            sent.append(send(piece, piece, g_ring_send.at[r, 1, e], g_recv.at[r, 1, e], at_y(3)))

    def g_to_mate(r, dy, slot, e):
        piece = g_piece(r, dy, False, e)
        sent.append(send(piece, piece, g_mate_send.at[r, slot, e], g_mate_recv.at[r, slot, e], mate))

    def g_first(r):
        for e in range(2):
            arrived(g_piece(r, 3, False, e), g_recv.at[r, 0, e])
            if e == 0:
                piece = g_piece(r, 3, False, 0)
                sent.append(send(piece, piece, g_fw_send.at[r, 0], g_recv.at[r, 2, 0], at_y(1)))
            arrived(g_piece(r, 1, False, 1 - e), g_recv.at[r, 1, 1 - e])
            if e == 0:
                piece = g_piece(r, 1, False, 1)
                sent.append(send(piece, piece, g_fw_send.at[r, 1], g_recv.at[r, 2, 1], at_y(3)))
            g_to_mate(r, 3, 1, e)
            g_to_mate(r, 1, 2, 1 - e)

    def g_second(r):
        for e in range(2):
            arrived(g_piece(r, 2, False, e), g_recv.at[r, 2, e])
            g_to_mate(r, 2, 3, e)

    def g_from_mate(r):
        for slot, dy in enumerate((0, 3, 1, 2)):
            for e in range(2):
                arrived(g_piece(r, dy, True, e), g_mate_recv.at[r, slot, e])

    for copy in g_copies:
        copy.wait()
    g_own(0)
    for r in range(4):
        for e in range(2):
            g_to_mate(r, 0, 0, e)
    g_own(1)

    def ring_own(ref, at, me, ag_send, recv, k):
        piece = ref.at[:, lanes(me, k)]
        arrived(piece, recv.at[0, k])
        sent.append(send(piece, piece, ag_send.at[0, k], recv.at[1, k], at(1)))
        sent.append(send(piece, piece, ag_send.at[1, k], recv.at[2, k], at(3)))

    def ring_forward(ref, at, me, fw_send, recv, k):
        if k < 2:
            piece, slot, to = ref.at[:, lanes((me + 3) % 4, k)], 1, at(1)
        else:
            piece, slot, to = ref.at[:, lanes((me + 1) % 4, k)], 2, at(3)
        arrived(piece, recv.at[slot, k])
        sent.append(send(piece, piece, fw_send.at[k], recv.at[3, k], to))

    def ring_rest(ref, me, recv):
        for k in range(4):
            if k >= 2:
                arrived(ref.at[:, lanes((me + 3) % 4, k)], recv.at[1, k])
            else:
                arrived(ref.at[:, lanes((me + 1) % 4, k)], recv.at[2, k])
        for k in range(4):
            arrived(ref.at[:, lanes((me + 2) % 4, k)], recv.at[3, k])

    for k in (0, 2, 1, 3):
        ring_own(w, at_z, z, w_ag_send, w_recv, k)
    for k in (0, 2, 1, 3):
        ring_own(tt, at_x, x, t_ag_send, t_recv, k)
    for k in (0, 2, 1, 3):
        ring_forward(w, at_z, z, w_fw_send, w_recv, k)
    g_first(0)
    g_own(2)
    for k in (0, 2, 1, 3):
        ring_forward(tt, at_x, x, t_fw_send, t_recv, k)
    g_second(0)
    g_first(1)
    g_own(3)
    ring_rest(w, z, w_recv)
    g_from_mate(0)

    def gi_tile(dx, j):
        rows = pl.ds(pl.multiple_of(((x + dx) % 4) * B, B), B)
        return lax.dot_general(
            g[rows, :], w[pl.ds(pl.multiple_of(j * TILE, TILE), TILE), :], (((1,), (1,)), ((), ())),
            preferred_element_type=F32,
        )

    def gw_tile(dz, j):
        rows = pl.ds(pl.multiple_of((j // 2) * B, B), B)
        columns = pl.ds(pl.multiple_of(((z + dz) % 4) * B + (j % 2) * TILE, TILE), TILE)
        return jnp.dot(tt[rows, :], g[:, columns], preferred_element_type=F32)

    class Reduction:
        def __init__(self, tile, at, tx, hop, rx, send_sem, hop_recv, recv):
            self.tile, self.at, self.tx, self.hop, self.rx = tile, at, tx, hop, rx
            self.send_sem, self.hop_recv, self.recv = send_sem, hop_recv, recv

        def far(self):
            @pl.loop(0, 4)
            def _(j):
                encode(self.tile(2, j), self.tx.at[0, j])
                send(self.tx.at[0, j], self.hop.at[j], self.send_sem.at[0, j], self.hop_recv.at[j], self.at(1 + 2 * (j // 2)))

        def near(self):
            @pl.loop(0, 4)
            def _(t):
                side, j = t // 2, (t + 2) % 4
                encode(self.tile(1 + 2 * side, j), self.tx.at[1 + side, j])
                send(
                    self.tx.at[1 + side, j], self.rx.at[side, j], self.send_sem.at[1 + side, j], self.recv.at[side, j],
                    self.at(1 + 2 * side),
                )

        def near_with_far(self):
            @pl.loop(0, 4)
            def _(j):
                side = j // 2
                tile = self.tile(1 + 2 * side, j)
                arrived(self.hop.at[j], self.hop_recv.at[j])
                encode(tile + decode(self.hop.at[j]), self.tx.at[1 + side, j])
                send(
                    self.tx.at[1 + side, j], self.rx.at[side, j], self.send_sem.at[1 + side, j], self.recv.at[side, j],
                    self.at(1 + 2 * side),
                )

        def total(self, j):
            tile = self.tile(0, j)
            for side in range(2):
                arrived(self.rx.at[side, j], self.recv.at[side, j])
                tile = tile + decode(self.rx.at[side, j])
            return tile.astype(BF16)

        def drain(self):
            @pl.loop(0, 4)
            def _(j):
                for k in range(3):
                    ref = self.tx.at[k, j]
                    pltpu.make_async_remote_copy(
                        src_ref=ref, dst_ref=ref, send_sem=self.send_sem.at[k, j], recv_sem=self.send_sem.at[k, j],
                        device_id=mate, device_id_type=MESH,
                    ).wait_send()

    gi = Reduction(gi_tile, at_x, gi_tx, gi_hop, gi_rx, gi_send, gi_hop_recv, gi_recv)
    gw = Reduction(gw_tile, at_z, gw_tx, gw_hop, gw_rx, gw_send, gw_hop_recv, gw_recv)

    gi.far()
    g_second(1)
    g_first(2)
    g_first(3)
    g_from_mate(1)
    g_second(2)
    g_from_mate(2)
    gi.near()
    g_second(3)
    ring_rest(tt, x, t_recv)
    g_from_mate(3)
    gw.far()
    gi.near_with_far()
    gw.near()
    gw.near_with_far()

    def gi_piece(j, k):
        columns = pl.ds(pl.multiple_of(k * 1024 + j * TILE, TILE), TILE)
        return gi_out.at[:, columns]

    @pl.loop(0, 4)
    def _(j):
        gi_fin[j] = gi.total(j)
        for k in range(4):
            send(
                gi_fin.at[j, pl.ds(k * 128, 128), :], gi_piece(j, q), gi_fin_send.at[j, k], gi_fin_recv.at[j, q], partner(k)
            )

    def gw_piece(i, k):
        return gw_out.at[pl.ds(pl.multiple_of(k * 1024 + i * B, B), B), :]

    @pl.loop(0, 4)
    def _(j):
        gw_fin[j] = gw.total(j)
        for e in range(2):
            send(
                gw_fin.at[j, :, pl.ds(e * 128, 128)], gw_piece(j // 2, q), gw_fin_send.at[j, e],
                gw_fin_recv.at[j // 2, q], partner(2 * (j % 2) + e),
            )

    for copy in sent:
        copy.wait_send()
    gi.drain()
    gw.drain()

    @pl.loop(0, 4)
    def _(j):
        for k in range(4):
            pltpu.make_async_remote_copy(
                src_ref=gi_fin.at[j, pl.ds(k * 128, 128), :], dst_ref=gi_piece(j, k), send_sem=gi_fin_send.at[j, k],
                recv_sem=gi_fin_recv.at[j, k], device_id=mate, device_id_type=MESH,
            ).wait()
        for e in range(2):
            pltpu.make_async_remote_copy(
                src_ref=gw_fin.at[j, :, pl.ds(e * 128, 128)], dst_ref=gw_piece(0, 0), send_sem=gw_fin_send.at[j, e],
                recv_sem=gw_fin_send.at[j, e], device_id=mate, device_id_type=MESH,
            ).wait_send()

    for i in range(2):
        for k in range(4):
            arrived(gw_piece(i, k), gw_fin_recv.at[i, k])


def per_device(tokens, weight, grad_output):
    dma = pltpu.SemaphoreType.DMA
    codes = lambda *lead: pltpu.VMEM((*lead, CODE_ROWS, TILE), BF16)
    any_spec = pl.BlockSpec(memory_space=pl.ANY)
    return pl.pallas_call(
        kernel,
        out_shape=(jax.ShapeDtypeStruct((128, 4096), BF16), jax.ShapeDtypeStruct((4096, 128), BF16)),
        in_specs=[any_spec] * 3,
        out_specs=(any_spec, any_spec),
        scratch_shapes=[
            pltpu.VMEM((128, 4096), BF16), pltpu.VMEM((4096, 128), BF16),
            pltpu.VMEM((1024, 2048), BF16), pltpu.VMEM((1024, 2048), BF16), pltpu.VMEM((2048, 2048), BF16),
            codes(3, 4), codes(4), codes(2, 4), codes(3, 4), codes(4), codes(2, 4),
            pltpu.VMEM((4, B, TILE), BF16), pltpu.VMEM((4, B, TILE), BF16),
            dma(()), dma((2,)),
            dma((4,)), dma((4,)), dma((2, 4)), dma((2, 4)), dma((4,)), dma((4,)), dma((4, 4)), dma((4, 4)),
            dma((4, 2, 2)), dma((4, 2)), dma((4, 4, 2)), dma((4, 3, 2)), dma((4, 4, 2)),
            dma((3, 4)), dma((4,)), dma((2, 4)), dma((3, 4)), dma((4,)), dma((2, 4)),
            dma((4, 4)), dma((4, 4)), dma((4, 2)), dma((2, 4)),
        ],
        compiler_params=pltpu.CompilerParams(
            collective_id=0, has_side_effects=True, vmem_limit_bytes=60 * 1024 * 1024
        ),
        name="linear_backward",
    )(tokens, weight, grad_output)


def solution(mesh):
    return jax.shard_map(
        per_device,
        mesh=mesh,
        in_specs=(P(("row", "col"), "depth"), P("depth", ("col", "row")), P("row", ("col", "depth"))),
        out_specs=(P(("row", "col"), "depth"), P("depth", ("col", "row"))),
        check_vma=False,
    )
```

time: 450 us -> 130 us (0.29)
  waiting for transfers between devices: 267 us -> 0 us
  blocking collectives: 125 us -> 0 us
  Pallas kernels: 0 us -> 124 us
  matrix products: 30.6 us -> 0 us
  between operations: 13.8 us -> 0.65 us
  other arithmetic: 7.92 us -> 0 us
    all_gather x2 -> x0, waiting for transfers between devices: 134 us -> none  [the longest x1 109 us: weight_grads(): lax.all_gather(tokens, 'col', axis=0, tiled=True)]
    reduce_scatter x1 -> x0, waiting for transfers between devices: 133 us -> none  [input_grads(): lax.psum_scatter(lax.dot_general(grad_block, weight_block, last_with_last...]
    all_to_all x2 -> x0, blocking collectives: 125 us -> none  [the longest x1 97.3 us: sum_at_owner(): lax.all_to_all(split_up(value, dim, devices), axis, 0, 0, tiled=True)]
    pallas_call x0 -> x1, Pallas kernels: none -> 124 us  [per_device(): pl.pallas_call(kernel, out_shape=(jax.ShapeDtypeStruct((128, 4096), BF16)...]
    dot_general x2 -> x0, matrix products: 30.6 us -> none  [the longest x1 18.4 us: input_grads(): lax.dot_general(grad_block, weight_block, last_with_last, preferred_eleme...]
    reduce_sum x1 -> x0, other arithmetic: 5.23 us -> none  [sum_at_owner(): return jnp.sum(blocks, axis=0)]
  transfers between devices with their start and end apart: 3 -> 0, of which waited for: 3 -> 0; matrix products, arithmetic and copies ran while one was open for 9% -> 0% of each run, Pallas kernels for 0% -> 0%
where the time goes in v1:
time: 130 us; the launch traced here: 128 us
  Pallas kernels  124 us (95%)
  local copies, waits for them, and re-layouts  3.35 us (3%)
    pallas_call x1, Pallas kernels, per_device(): pl.pallas_call(kernel, out_shape=(jax.ShapeDtypeStruct((128, 4096), BF16)...  124 us
    unnamed x4, local copies, waits for them, and re-layouts  3.35 us

profile of v1, /device:TPU:1, one launch (start us, length us, event | category | flops | bytes accessed | tf_op | source)
XLA Modules:
  0.0 127.6 jit_solution(11468887632309361652)
XLA Ops:
  0.6 123.6 %linear_backward.1 = (bf16[128,4096]{1,0:T(8,128)(2,1)}, bf16[4096,128]{1,0:T(8,128)(2,1)}) custom-call(bf16[128,4096]{1,0:T(8,128)(2,1)} %t_hbm.1, bf16[4096,128]{1,0:T(8,128)(2,1)} %w_hbm.1, bf16[2048,256]{1,0:T(8,128)(2,1)} %g_hbm.1), custom_call_target="tpu_custom_call" | custom-call | tf_op jit(solution)/shard_map/linear_backward/pallas_call | solution.py:329
  124.2 0.0 copy-start
  124.2 2.4 %copy.7 = bf16[128,4096]{1,0:T(8,128)(2,1)} copy(bf16[128,4096]{1,0:T(8,128)(2,1)} %get-tuple-element.4) | data formatting | bytes 2097152
  126.6 0.0 copy-done
  126.6 1.0 copy.8
Async XLA Ops:
  124.2 2.4 %copy-start = (bf16[4096,128]{1,0:T(8,128)(2,1)S(1)}, bf16[4096,128]{1,0:T(8,128)(2,1)}, u32[]{:S(2)}) copy-start(bf16[4096,128]{1,0:T(8,128)(2,1)} %get-tuple-element.5) | copy-start | bytes 3145732

commit v2 on v0

v2 whole, which is shorter than its diff:
```python
import jax
import jax.numpy as jnp
from jax import lax
from jax.experimental import pallas as pl
from jax.experimental.pallas import tpu as pltpu
from jax.sharding import PartitionSpec as P

MESH = pl.DeviceIdType.MESH
BF16, F32 = jnp.bfloat16, jnp.float32

B = 512
TILE = 256
CODE_ROWS = B + 16
TOP = 320.0
POWER = 15
PARTS = 4
PART = 1024 // PARTS

OWN, RIGHT, FAR, LEFT = 0, 1, 2, 3
TOKEN_SLOT = {FAR: 0, RIGHT: 1, LEFT: 2, OWN: 3}


def weight_lane(member, pair):
    return {FAR: 0, OWN: 256, RIGHT: 1024, LEFT: 1280}[member] + pair * 512


def token_lane(member, pair):
    return TOKEN_SLOT[member] * B + pair * 256


def encode(tile, ref):
    top = jnp.max(jnp.abs(tile), axis=0, keepdims=True)
    scale = (top * 1.01 + 1e-30).astype(BF16)
    u = tile * (TOP / scale.astype(F32))
    u3 = u * u * u
    u6 = u3 * u3
    ref[0:B, :] = (u6 * u6 * u3).astype(BF16)
    ref[B:CODE_ROWS, :] = jnp.broadcast_to(scale.astype(F32), (16, TILE)).astype(BF16)


def decode(ref):
    code = ref[0:B, :].astype(F32)
    scale = ref[B:CODE_ROWS, :].astype(F32)[0:1] * (1.0 / TOP)
    size = jnp.exp2(jnp.log2(jnp.abs(code)) * (1.0 / POWER))
    return jnp.where(code < 0, -size, size) * scale


class Reduction:
    def __init__(self, send, arrived, at, far_tx, hop, tx, rx, far_send, hop_recv, send_sem, recv):
        self.send, self.arrived, self.at, self.far_tx, self.hop, self.tx, self.rx = send, arrived, at, far_tx, hop, tx, rx
        self.far_send, self.hop_recv, self.send_sem, self.recv = far_send, hop_recv, send_sem, recv

    def half(self, ref, j, side):
        return ref.at[j, :, pl.ds(side * 128, 128)]

    def far(self, tile, j):
        encode(tile, self.far_tx.at[j])

    def far_start(self, j):
        for side in range(2):
            self.send(
                self.half(self.far_tx, j, side), self.half(self.hop, j, side), self.far_send,
                self.hop_recv.at[side, j], self.at(1 + 2 * side),
            )

    def near_wait(self, j):
        for side in range(2):
            self.arrived(self.half(self.hop, j, side), self.hop_recv.at[side, j])

    def near(self, tile, j, side):
        parts = [tile[:, 0:128], tile[:, 128:256]]
        parts[side] = parts[side] + decode(self.half(self.hop, j, side))
        encode(jnp.concatenate(parts, axis=1), self.tx.at[side, j])

    def near_start(self, j):
        for side in range(2):
            self.send(
                self.tx.at[side, j], self.rx.at[side, j], self.send_sem, self.recv.at[side, j],
                self.at(1 + 2 * side),
            )

    def total_wait(self, j):
        for side in range(2):
            self.arrived(self.rx.at[side, j], self.recv.at[side, j])

    def total(self, tile, j):
        return (tile + decode(self.rx.at[0, j]) + decode(self.rx.at[1, j])).astype(BF16)

    def drain(self, sent_from):
        sent_from(self.far_tx, self.far_send)
        sent_from(self.tx, self.send_sem)


def kernel(
    t_hbm, w_hbm, g_hbm, gi_all, gw_all,
    t_loc, tt_loc, tt, w, g, gi_far_tx, gi_hop, gi_tx, gi_rx, gw_far_tx, gw_hop, gw_tx, gw_rx, gi_fin, gw_fin, gw_own, gi_own, gi_part, gw_part,
    local_sem, g_local_sem,
    w_ex_send, t_ex_send, w_ex_recv, t_ex_recv, w_ag_send, t_ag_send, w_fw_send, t_fw_send, w_recv, t_recv, w_rest, t_rest,
    g_ring_send, g_fw_send, g_mate_send, g_recv, g_mate_recv,
    gi_far_send, gi_hop_recv, gi_send, gi_recv, gw_far_send, gw_hop_recv, gw_send, gw_recv,
    gi_fin_send, gi_fin_recv, gw_fin_send, gw_fin_recv,
):
    z, col, yl = lax.axis_index("row"), lax.axis_index("col"), lax.axis_index("depth")
    x, q = col // 4, col % 4
    yh, core = q // 2, q % 2
    y = 2 * yh + yl

    def at_x(k):
        return (z, ((x + k) % 4) * 4 + q, yl)

    def at_z(k):
        return ((z + k) % 4, col, yl)

    def at_y(k):
        other = (y + k) % 4
        return (z, x * 4 + (other // 2) * 2 + core, other % 2)

    mate = (z, x * 4 + yh * 2 + (1 - core), yl)

    def partner(k):
        return (z, x * 4 + k, 1 - yl)

    def send(src, dst, send_sem, recv_sem, to):
        copy = pltpu.make_async_remote_copy(
            src_ref=src, dst_ref=dst, send_sem=send_sem, recv_sem=recv_sem, device_id=to, device_id_type=MESH
        )
        copy.start()

    def arrived(ref, sem):
        pltpu.make_async_remote_copy(
            src_ref=ref, dst_ref=ref, send_sem=sem, recv_sem=sem, device_id=mate, device_id_type=MESH
        ).wait_recv()

    def sent_from(ref, sem):
        pltpu.make_async_remote_copy(
            src_ref=ref, dst_ref=ref, send_sem=sem, recv_sem=sem, device_id=mate, device_id_type=MESH
        ).wait_send()

    steps = ((FAR, 0), (FAR, 1), (RIGHT, 0), (LEFT, 0), (OWN, 0), (RIGHT, 1), (LEFT, 1), (OWN, 1))

    def g_lane(owner, owner_core, late):
        member = (2 * (owner % 2) + (z + late) % 2 - z + 4) % 4
        second = (1 - member // 2) if late == 0 else member // 2
        return pl.multiple_of(late * 1024 + (owner // 2) * 512 + second * 256 + owner_core * 128, 128)

    def g_piece(s, dy, other_core=False, half=None):
        member, late = steps[s]
        start, size = TOKEN_SLOT[member] * B, B
        if half is not None:
            start, size = start + half * (B // 2), B // 2
        lane = g_lane((y + dy) % 4, (1 - core) if other_core else core, late)
        return g.at[pl.ds(start, size), pl.ds(lane, 128)]

    t_copy = pltpu.make_async_copy(t_hbm, t_loc, local_sem)
    t_copy.start()
    for s, (member, late) in enumerate(steps):
        rows = pl.ds(pl.multiple_of(((x + member) % 4) * B, B), B)
        columns = pl.ds(pl.multiple_of(((z + late) % 2) * 128, 128), 128)
        pltpu.make_async_copy(g_hbm.at[rows, columns], g_piece(s, 0), g_local_sem).start()

    barrier = pltpu.get_barrier_semaphore()
    peers = [at_x(1), at_x(3), at_z(1), at_z(3), mate] + [partner(k) for k in range(4)]
    for peer in peers:
        pl.semaphore_signal(barrier, inc=1, device_id=peer, device_id_type=MESH)
    with jax.named_scope("s00_barrier"):
        pl.semaphore_wait(barrier, len(peers))

    def part_rows(part):
        return pl.ds(part * PART, PART)

    def exchange(src, ref, lane, ex_send, ex_recv, part):
        for k in range(4):
            piece = src.at[pl.ds(k * 1024 + part * PART, PART), :]
            send(piece, ref.at[part_rows(part), pl.ds(lane, 128)], ex_send, ex_recv.at[part, q // 2], partner(k))

    w_own_lane = pl.multiple_of((q // 2) * 512 + 256 + (q % 2) * 128, 128)
    t_own_lane = pl.multiple_of(TOKEN_SLOT[OWN] * B + q * 128, 128)
    exchange(w_hbm, w, w_own_lane, w_ex_send, w_ex_recv, 0)
    t_copy.wait()
    for k in range(8):
        tt_loc[k * 512 : k * 512 + 512, :] = t_loc[:, k * 512 : k * 512 + 512].T
    exchange(tt_loc, tt, t_own_lane, t_ex_send, t_ex_recv, 0)
    for part in range(1, PARTS):
        exchange(w_hbm, w, w_own_lane, w_ex_send, w_ex_recv, part)
        exchange(tt_loc, tt, t_own_lane, t_ex_send, t_ex_recv, part)

    def g_own(s):
        piece = g_piece(s, 0)
        send(piece, piece, g_ring_send, g_recv.at[s, 0], at_y(1))
        send(piece, piece, g_ring_send, g_recv.at[s, 1], at_y(3))

    def g_to_mate(s, dy):
        piece = g_piece(s, dy)
        send(piece, piece, g_mate_send, g_mate_recv.at[s], mate)

    def g_first(s):
        for side, dy in ((0, 3), (1, 1)):
            arrived(g_piece(s, dy), g_recv.at[s, side])
            piece = g_piece(s, dy, half=side)
            send(piece, piece, g_fw_send, g_recv.at[s, 2], at_y(1 + 2 * side))
            g_to_mate(s, dy)

    def g_second(s):
        arrived(g_piece(s, 2), g_recv.at[s, 2])
        g_to_mate(s, 2)

    def g_from_mate(s):
        arrived(g.at[0:B, 0:512], g_mate_recv.at[s])

    pltpu.make_async_copy(tt_loc, tt_loc, g_local_sem).wait()
    g_own(0)
    for s in range(8):
        g_to_mate(s, 0)
    g_own(1)

    class Ring:
        def __init__(self, ref, lane, at, ex_recv, ag_send, fw_send, recv, rest_recv):
            self.ref, self.lane, self.at = ref, lane, at
            self.ex_recv, self.ag_send, self.fw_send, self.recv, self.rest_recv = ex_recv, ag_send, fw_send, recv, rest_recv

        def piece(self, member, part, pair):
            return self.ref.at[part_rows(part), pl.ds(self.lane(member, pair), 256)]

        def own(self, part):
            for pair in range(2):
                piece = self.piece(OWN, part, pair)
                arrived(piece, self.ex_recv.at[part, pair])
                for side, member in ((0, LEFT), (1, RIGHT)):
                    kept = (part < PARTS // 2) == (side == 1)
                    sem = self.rest_recv.at[0] if kept else self.recv.at[part, pair]
                    send(piece, self.piece(member, part, pair), self.ag_send, sem, self.at(1 + 2 * side))

        def forward(self, part):
            side = 0 if part < PARTS // 2 else 1
            for pair in range(2):
                piece = self.piece((LEFT, RIGHT)[side], part, pair)
                arrived(piece, self.recv.at[part, pair])
                send(piece, self.piece(FAR, part, pair), self.fw_send, self.rest_recv.at[1], self.at(1 + 2 * side))

        def rest(self):
            for k in range(2):
                arrived(self.ref.at[:, 0:512], self.rest_recv.at[k])

        def drain(self):
            sent_from(self.ref.at[:, 0:1024], self.ag_send)
            sent_from(self.ref.at[:, 0:512], self.fw_send)

    w_ring = Ring(w, weight_lane, at_z, w_ex_recv, w_ag_send, w_fw_send, w_recv, w_rest)
    t_ring = Ring(tt, token_lane, at_x, t_ex_recv, t_ag_send, t_fw_send, t_recv, t_rest)

    with jax.named_scope("s02_own01"):
        w_ring.own(0)
        t_ring.own(0)
        w_ring.own(1)
    with jax.named_scope("s03_own12"):
        t_ring.own(1)
        w_ring.forward(0)
        w_ring.own(2)
        t_ring.forward(0)
        t_ring.own(2)
    with jax.named_scope("s04_own3"):
        w_ring.forward(1)
        w_ring.own(3)
        t_ring.forward(1)
        t_ring.own(3)
    with jax.named_scope("s05_wfw2"):
        w_ring.forward(2)
    with jax.named_scope("s08_g0"):
        g_first(0)
        g_own(2)
    with jax.named_scope("s09_tfw2wfw3"):
        t_ring.forward(2)
        w_ring.forward(3)
    with jax.named_scope("s10_g1"):
        g_first(1)
        g_own(3)
        g_second(0)
    with jax.named_scope("s11_tfw3"):
        t_ring.forward(3)
    with jax.named_scope("s12_g2"):
        g_first(2)
        g_own(4)
        g_second(1)
    with jax.named_scope("s13_g3"):
        g_first(3)
        g_own(5)
        g_second(2)
    with jax.named_scope("s14_wrest"):
        w_ring.rest()
    with jax.named_scope("s15_gm01"):
        g_from_mate(0)
        g_from_mate(1)

    by_rows = (((1,), (1,)), ((), ()))

    HALF = 1024

    def gi_dot(slot, slots, j, tiles, first=0, terms=2 * HALF):
        return lax.dot_general(
            g[slot * B : (slot + slots) * B, first : first + terms],
            w[pl.ds(pl.multiple_of(j * TILE, TILE), tiles * TILE), first : first + terms],
            by_rows, preferred_element_type=F32,
        )

    def gw_dot(lane, j, first=0, terms=2 * HALF):
        rows = pl.ds(pl.multiple_of((j // 2) * B, B), B)
        columns = pl.ds(pl.multiple_of(lane + (j % 2) * 512, 512), 512)
        return jnp.dot(tt[rows, first : first + terms], g[first : first + terms, columns], preferred_element_type=F32)

    gi = Reduction(send, arrived, at_x, gi_far_tx, gi_hop, gi_tx, gi_rx, gi_far_send, gi_hop_recv, gi_send, gi_recv)
    gw = Reduction(send, arrived, at_z, gw_far_tx, gw_hop, gw_tx, gw_rx, gw_far_send, gw_hop_recv, gw_send, gw_recv)

    def gi_far_pair(j):
        both = gi_dot(0, 1, j, 2)
        for k in range(2):
            gi.far(both[:, k * TILE : (k + 1) * TILE], j + k)
        for k in range(2):
            gi.far_start(j + k)

    def gw_columns_dot(lane, half):
        columns = pl.ds(pl.multiple_of(lane + half * 512, 256), TILE)
        return jnp.dot(tt[...], g[:, columns], preferred_element_type=F32)

    def gw_far_pair(half):
        columns = pl.ds(pl.multiple_of(half * 512, 256), TILE)
        for k in range(2):
            tile = jnp.dot(tt[k * B : (k + 1) * B, :], g[:, columns], preferred_element_type=F32)
            gw.far(tile, 2 * k + half)
        for k in range(2):
            gw.far_start(2 * k + half)

    def gw_own_all():
        @pl.loop(0, 2)
        def _(half):
            both = gw_columns_dot(TILE, half)
            for k in range(2):
                gw_own[2 * k + half] = both[k * B : (k + 1) * B]

    def gi_near_part(h):
        both = gi_dot(1, 2, 2 * h, 2, 0, HALF)
        for side in range(2):
            for k in range(2):
                gi_part[side, 2 * h + k] = both[side * B : (side + 1) * B, k * TILE : (k + 1) * TILE]

    def gi_own_part():
        @pl.loop(0, 2)
        def _(h):
            both = gi_dot(3, 1, 2 * h, 2, 0, HALF)
            for k in range(2):
                gi_own[2 * h + k] = both[:, k * TILE : (k + 1) * TILE]

    def gw_near_part(j):
        gw_part[j] = gw_dot(1024, j, 0, HALF)

    def gi_near(j):
        gi.near_wait(j)
        for side in range(2):
            tile = gi_part[side, j] + gi_dot(1 + side, 1, j, 1, HALF, HALF)
            gi.near(tile, j, side)
        gi.near_start(j)

    def gw_near(j):
        gw.near_wait(j)
        both = gw_part[j] + gw_dot(1024, j, HALF, HALF)
        for side in range(2):
            gw.near(both[:, side * TILE : (side + 1) * TILE], j, side)
        gw.near_start(j)

    def gi_piece(j, k):
        return gi_all.at[:, pl.ds(pl.multiple_of(k * 1024 + j * TILE, TILE), TILE)]

    def gw_piece(i, k):
        return gw_all.at[pl.ds(pl.multiple_of(k * 1024 + i * B, B), B), :]

    def gi_final(j):
        tile = gi_own[j] + gi_dot(3, 1, j, 1, HALF, HALF)
        gi.total_wait(j)
        gi_fin[j] = gi.total(tile, j)
        for k in range(4):
            send(
                gi_fin.at[j, pl.ds(k * 128, 128), :], gi_piece(j, q), gi_fin_send, gi_fin_recv,
                partner(k),
            )

    def gw_final(j):
        gw.total_wait(j)
        gw_fin[j] = gw.total(gw_own[j], j)
        for e in range(2):
            send(
                gw_fin.at[j, :, pl.ds(e * 128, 128)], gw_piece(j // 2, q), gw_fin_send,
                gw_fin_recv, partner(2 * (j % 2) + e),
            )

    def steps_of(count, work, after, name):
        @pl.loop(0, count)
        def _(h):
            with jax.named_scope(name):
                work(h)
            for at, service in after.items():

                @pl.when(h == at)
                def _():
                    with jax.named_scope(name + "_g"):
                        service()

    def forward_4():
        g_first(4)
        g_own(6)

    def forward_5():
        g_first(5)
        g_own(7)

    steps_of(2, lambda h: gi_far_pair(2 * h), {0: forward_4, 1: lambda: g_second(3)}, "s16_gifar")
    with jax.named_scope("s17_gm23"):
        g_from_mate(2)
        g_from_mate(3)
    steps_of(2, gi_near_part, {0: forward_5, 1: lambda: g_second(4)}, "s18_gipart")
    with jax.named_scope("s19_trest"):
        t_ring.rest()
        g_from_mate(4)
    steps_of(2, gw_far_pair, {0: lambda: g_first(6), 1: lambda: g_second(5)}, "s20_gwfar")
    with jax.named_scope("s21_gm5"):
        g_from_mate(5)
    steps_of(4, gw_near_part, {1: lambda: g_first(7), 3: lambda: g_second(6)}, "s22_gwpart")
    with jax.named_scope("s23_giown"):
        gi_own_part()
    with jax.named_scope("s24_g7"):
        g_second(7)
        g_from_mate(6)

    @pl.loop(0, 5)
    def _(j):
        @pl.when(j < 4)
        def _():
            with jax.named_scope("s31_ginear"):
                gi_near(j)

        @pl.when(j == 0)
        def _():
            with jax.named_scope("s30_gm7"):
                g_from_mate(7)

        @pl.when(j < 4)
        def _():
            with jax.named_scope("s33_gwnear"):
                gw_near(j)

        @pl.when(j == 1)
        def _():
            with jax.named_scope("s34_gwown"):
                gw_own_all()

        @pl.when(j > 0)
        def _():
            with jax.named_scope("s35_gifinal"):
                gi_final(j - 1)
            with jax.named_scope("s36_gwfinal"):
                gw_final(j - 1)

    with jax.named_scope("s50_drain"):
        for src, sem in ((w_hbm, w_ex_send), (tt_loc, t_ex_send), (gi_fin, gi_fin_send), (gw_fin, gw_fin_send)):
            sent_from(src, sem)
        sent_from(g.at[0:B, :], g_ring_send)
        sent_from(g.at[0:B, 0:1024], g_fw_send)
        sent_from(g.at[:, 0:1024], g_mate_send)
        w_ring.drain()
        t_ring.drain()
        gi.drain(sent_from)
        gw.drain(sent_from)
    with jax.named_scope("s52_giout"):
        arrived(gi_all, gi_fin_recv)
    with jax.named_scope("s53_gwout"):
        arrived(gw_all, gw_fin_recv)


def per_device(tokens, weight, grad_output):
    dma = pltpu.SemaphoreType.DMA
    codes = lambda *lead: pltpu.VMEM((*lead, CODE_ROWS, TILE), BF16)
    any_spec = pl.BlockSpec(memory_space=pl.ANY)
    return pl.pallas_call(
        kernel,
        out_shape=(pltpu.VMEM((128, 4096), BF16), pltpu.VMEM((4096, 128), BF16)),
        in_specs=[any_spec] * 3,
        out_specs=(any_spec, any_spec),
        scratch_shapes=[
            pltpu.VMEM((128, 4096), BF16), pltpu.VMEM((4096, 128), BF16),
            pltpu.VMEM((1024, 2048), BF16), pltpu.VMEM((1024, 2048), BF16), pltpu.VMEM((2048, 2048), BF16),
            codes(4), codes(4), codes(2, 4), codes(2, 4), codes(4), codes(4), codes(2, 4), codes(2, 4),
            pltpu.VMEM((4, B, TILE), BF16), pltpu.VMEM((4, B, TILE), BF16), pltpu.VMEM((4, B, TILE), F32),
            pltpu.VMEM((4, B, TILE), F32), pltpu.VMEM((2, 4, B, TILE), F32), pltpu.VMEM((4, B, 2 * TILE), F32),
            dma(()), dma(()),
            dma(()), dma(()), dma((PARTS, 2)), dma((PARTS, 2)),
            dma(()), dma(()), dma(()), dma(()), dma((PARTS, 2)), dma((PARTS, 2)), dma((2,)), dma((2,)),
            dma(()), dma(()), dma(()), dma((8, 3)), dma((8,)),
            dma(()), dma((2, 4)), dma(()), dma((2, 4)), dma(()), dma((2, 4)), dma(()), dma((2, 4)),
            dma(()), dma(()), dma(()), dma(()),
        ],
        compiler_params=pltpu.CompilerParams(
            collective_id=0, has_side_effects=True, vmem_limit_bytes=58 * 1024 * 1024
        ),
        name="linear_backward",
    )(tokens, weight, grad_output)


def solution(mesh):
    return jax.shard_map(
        per_device,
        mesh=mesh,
        in_specs=(P(("row", "col"), "depth"), P("depth", ("col", "row")), P("row", ("col", "depth"))),
        out_specs=(P(("row", "col"), "depth"), P("depth", ("col", "row"))),
        check_vma=False,
    )
```

time: 450 us -> 108 us (0.24)
  waiting for transfers between devices: 267 us -> 0 us
  blocking collectives: 125 us -> 0 us
  Pallas kernels: 0 us -> 105 us
  matrix products: 30.6 us -> 0 us
  between operations: 13.8 us -> 0.64 us
  other arithmetic: 7.92 us -> 0 us
    all_gather x2 -> x0, waiting for transfers between devices: 134 us -> none  [the longest x1 109 us: weight_grads(): lax.all_gather(tokens, 'col', axis=0, tiled=True)]
    reduce_scatter x1 -> x0, waiting for transfers between devices: 133 us -> none  [input_grads(): lax.psum_scatter(lax.dot_general(grad_block, weight_block, last_with_last...]
    all_to_all x2 -> x0, blocking collectives: 125 us -> none  [the longest x1 97.3 us: sum_at_owner(): lax.all_to_all(split_up(value, dim, devices), axis, 0, 0, tiled=True)]
    pallas_call x0 -> x1, Pallas kernels: none -> 105 us  [per_device(): pl.pallas_call(kernel, out_shape=(pltpu.VMEM((128, 4096), BF16), pltpu.VM...]
    dot_general x2 -> x0, matrix products: 30.6 us -> none  [the longest x1 18.4 us: input_grads(): lax.dot_general(grad_block, weight_block, last_with_last, preferred_eleme...]
    reduce_sum x1 -> x0, other arithmetic: 5.23 us -> none  [sum_at_owner(): return jnp.sum(blocks, axis=0)]
  transfers between devices with their start and end apart: 3 -> 0, of which waited for: 3 -> 0; matrix products, arithmetic and copies ran while one was open for 9% -> 0% of each run, Pallas kernels for 0% -> 0%
where the time goes in v2:
time: 108 us
  Pallas kernels  105 us (97%)
  local copies, waits for them, and re-layouts  1.94 us (2%)
    pallas_call x1, Pallas kernels, per_device(): pl.pallas_call(kernel, out_shape=(pltpu.VMEM((128, 4096), BF16), pltpu.VM...  105 us

profile of v2, /device:TPU:1, one launch (start us, length us, event | category | flops | bytes accessed | tf_op | source)
XLA Modules:
  0.0 107.6 jit_solution(15324963151194993884)
XLA Ops:
  0.6 105.0 %linear_backward.1 = (bf16[128,4096]{1,0:T(8,128)(2,1)S(1)}, bf16[4096,128]{1,0:T(8,128)(2,1)S(1)}) custom-call(bf16[128,4096]{1,0:T(8,128)(2,1)} %t_hbm.1, bf16[4096,128]{1,0:T(8,128)(2,1)} %w_hbm.1, bf16[2048,256]{1,0:T(8,128)(2,1)} %g_hbm.1), custom_call_target="tpu_custom_call" | custom-call | tf_op jit(solution)/shard_map/linear_backward/pallas_call | solution.py:481
  105.7 1.0 copy.7
  106.7 1.0 copy.8

commit v3 on v2

--- a/solution.py
+++ b/solution.py
@@ -10,7 +10,7 @@
 
 B = 512
 TILE = 256
-CODE_ROWS = B + 16
+CODE_ROWS = B + 8
 TOP = 320.0
 POWER = 15
 PARTS = 4
@@ -35,7 +35,7 @@
     u3 = u * u * u
     u6 = u3 * u3
     ref[0:B, :] = (u6 * u6 * u3).astype(BF16)
-    ref[B:CODE_ROWS, :] = jnp.broadcast_to(scale.astype(F32), (16, TILE)).astype(BF16)
+    ref[B:CODE_ROWS, :] = jnp.broadcast_to(scale.astype(F32), (8, tile.shape[1])).astype(BF16)
 
 
 def decode(ref):
@@ -63,28 +63,25 @@
                 self.hop_recv.at[side, j], self.at(1 + 2 * side),
             )
 
-    def near_wait(self, j):
-        for side in range(2):
-            self.arrived(self.half(self.hop, j, side), self.hop_recv.at[side, j])
+    def near_wait(self, j, side):
+        self.arrived(self.half(self.hop, j, side), self.hop_recv.at[side, j])
 
     def near(self, tile, j, side):
         parts = [tile[:, 0:128], tile[:, 128:256]]
         parts[side] = parts[side] + decode(self.half(self.hop, j, side))
         encode(jnp.concatenate(parts, axis=1), self.tx.at[side, j])
 
-    def near_start(self, j):
+    def near_start(self, j, side):
+        for e in range(2):
+            self.send(
+                self.half(self.tx.at[side], j, e), self.half(self.rx.at[side], j, e), self.send_sem,
+                self.recv.at[side, j, e], self.at(1 + 2 * side),
+            )
+
+    def total(self, own, j, e):
         for side in range(2):
-            self.send(
-                self.tx.at[side, j], self.rx.at[side, j], self.send_sem, self.recv.at[side, j],
-                self.at(1 + 2 * side),
-            )
-
-    def total_wait(self, j):
-        for side in range(2):
-            self.arrived(self.rx.at[side, j], self.recv.at[side, j])
-
-    def total(self, tile, j):
-        return (tile + decode(self.rx.at[0, j]) + decode(self.rx.at[1, j])).astype(BF16)
+            self.arrived(self.half(self.rx.at[side], j, e), self.recv.at[side, j, e])
+        return (own + decode(self.half(self.rx.at[0], j, e)) + decode(self.half(self.rx.at[1], j, e))).astype(BF16)
 
     def drain(self, sent_from):
         sent_from(self.far_tx, self.far_send)
@@ -93,8 +90,8 @@
 
 def kernel(
     t_hbm, w_hbm, g_hbm, gi_all, gw_all,
-    t_loc, tt_loc, tt, w, g, gi_far_tx, gi_hop, gi_tx, gi_rx, gw_far_tx, gw_hop, gw_tx, gw_rx, gi_fin, gw_fin, gw_own, gi_own, gi_part, gw_part,
-    local_sem, g_local_sem,
+    t_loc, w_loc, tt_loc, tt, w, g, gi_far_tx, gi_hop, gi_tx, gi_rx, gw_far_tx, gw_hop, gw_tx, gw_rx, gi_fin, gw_fin, gw_fin_own, gi_own, gi_part, gw_part,
+    local_sem, w_local_sem, g_local_sem,
     w_ex_send, t_ex_send, w_ex_recv, t_ex_recv, w_ag_send, t_ag_send, w_fw_send, t_fw_send, w_recv, t_recv, w_rest, t_rest,
     g_ring_send, g_fw_send, g_mate_send, g_recv, g_mate_recv,
     gi_far_send, gi_hop_recv, gi_send, gi_recv, gw_far_send, gw_hop_recv, gw_send, gw_recv,
@@ -151,6 +148,8 @@
         lane = g_lane((y + dy) % 4, (1 - core) if other_core else core, late)
         return g.at[pl.ds(start, size), pl.ds(lane, 128)]
 
+    w_copy = pltpu.make_async_copy(w_hbm, w_loc, w_local_sem)
+    w_copy.start()
     t_copy = pltpu.make_async_copy(t_hbm, t_loc, local_sem)
     t_copy.start()
     for s, (member, late) in enumerate(steps):
@@ -175,13 +174,14 @@
 
     w_own_lane = pl.multiple_of((q // 2) * 512 + 256 + (q % 2) * 128, 128)
     t_own_lane = pl.multiple_of(TOKEN_SLOT[OWN] * B + q * 128, 128)
-    exchange(w_hbm, w, w_own_lane, w_ex_send, w_ex_recv, 0)
+    w_copy.wait()
+    exchange(w_loc, w, w_own_lane, w_ex_send, w_ex_recv, 0)
     t_copy.wait()
     for k in range(8):
         tt_loc[k * 512 : k * 512 + 512, :] = t_loc[:, k * 512 : k * 512 + 512].T
     exchange(tt_loc, tt, t_own_lane, t_ex_send, t_ex_recv, 0)
     for part in range(1, PARTS):
-        exchange(w_hbm, w, w_own_lane, w_ex_send, w_ex_recv, part)
+        exchange(w_loc, w, w_own_lane, w_ex_send, w_ex_recv, part)
         exchange(tt_loc, tt, t_own_lane, t_ex_send, t_ex_recv, part)
 
     def g_own(s):
@@ -193,12 +193,19 @@
         piece = g_piece(s, dy)
         send(piece, piece, g_mate_send, g_mate_recv.at[s], mate)
 
-    def g_first(s):
+    def g_forward(s):
         for side, dy in ((0, 3), (1, 1)):
             arrived(g_piece(s, dy), g_recv.at[s, side])
             piece = g_piece(s, dy, half=side)
             send(piece, piece, g_fw_send, g_recv.at[s, 2], at_y(1 + 2 * side))
+
+    def g_first_to_mate(s):
+        for dy in (3, 1):
             g_to_mate(s, dy)
+
+    def g_first(s):
+        g_forward(s)
+        g_first_to_mate(s)
 
     def g_second(s):
         arrived(g_piece(s, 2), g_recv.at[s, 2])
@@ -317,24 +324,17 @@
         for k in range(2):
             gi.far_start(j + k)
 
-    def gw_columns_dot(lane, half):
-        columns = pl.ds(pl.multiple_of(lane + half * 512, 256), TILE)
-        return jnp.dot(tt[...], g[:, columns], preferred_element_type=F32)
-
-    def gw_far_pair(half):
-        columns = pl.ds(pl.multiple_of(half * 512, 256), TILE)
-        for k in range(2):
-            tile = jnp.dot(tt[k * B : (k + 1) * B, :], g[:, columns], preferred_element_type=F32)
-            gw.far(tile, 2 * k + half)
-        for k in range(2):
-            gw.far_start(2 * k + half)
-
-    def gw_own_all():
-        @pl.loop(0, 2)
-        def _(half):
-            both = gw_columns_dot(TILE, half)
-            for k in range(2):
-                gw_own[2 * k + half] = both[k * B : (k + 1) * B]
+    def gw_far(t):
+        j = 2 * (t % 2) + t // 2
+        rows = pl.ds(pl.multiple_of((t % 2) * B, B), B)
+        columns = pl.ds(pl.multiple_of((t // 2) * 512, 512), TILE)
+        gw.far(jnp.dot(tt[rows, :], g[:, columns], preferred_element_type=F32), j)
+        gw.far_start(j)
+
+    def gw_own(j):
+        rows = pl.ds(pl.multiple_of((j // 2) * B, B), B)
+        columns = pl.ds(pl.multiple_of((j % 2) * 512 + TILE, TILE), TILE)
+        return jnp.dot(tt[rows, :], g[:, columns], preferred_element_type=F32)
 
     def gi_near_part(h):
         both = gi_dot(1, 2, 2 * h, 2, 0, HALF)
@@ -342,29 +342,30 @@
             for k in range(2):
                 gi_part[side, 2 * h + k] = both[side * B : (side + 1) * B, k * TILE : (k + 1) * TILE]
 
-    def gi_own_part():
+    def gi_own_all():
         @pl.loop(0, 2)
         def _(h):
-            both = gi_dot(3, 1, 2 * h, 2, 0, HALF)
+            both = gi_dot(3, 1, 2 * h, 2)
             for k in range(2):
                 gi_own[2 * h + k] = both[:, k * TILE : (k + 1) * TILE]
 
     def gw_near_part(j):
         gw_part[j] = gw_dot(1024, j, 0, HALF)
 
-    def gi_near(j):
-        gi.near_wait(j)
+    def gi_near(j, side):
+        gi.near_wait(j, side)
+        tile = gi_part[side, j] + gi_dot(1 + side, 1, j, 1, HALF, HALF)
+        gi.near(tile, j, side)
+        gi.near_start(j, side)
+
+    def gw_near(j):
         for side in range(2):
-            tile = gi_part[side, j] + gi_dot(1 + side, 1, j, 1, HALF, HALF)
-            gi.near(tile, j, side)
-        gi.near_start(j)
-
-    def gw_near(j):
-        gw.near_wait(j)
+            gw.near_wait(j, side)
         both = gw_part[j] + gw_dot(1024, j, HALF, HALF)
         for side in range(2):
             gw.near(both[:, side * TILE : (side + 1) * TILE], j, side)
-        gw.near_start(j)
+        for side in range(2):
+            gw.near_start(j, side)
 
     def gi_piece(j, k):
         return gi_all.at[:, pl.ds(pl.multiple_of(k * 1024 + j * TILE, TILE), TILE)]
@@ -373,22 +374,20 @@
         return gw_all.at[pl.ds(pl.multiple_of(k * 1024 + i * B, B), B), :]
 
     def gi_final(j):
-        tile = gi_own[j] + gi_dot(3, 1, j, 1, HALF, HALF)
-        gi.total_wait(j)
-        gi_fin[j] = gi.total(tile, j)
+        for e in range(2):
+            columns = slice(e * 128, (e + 1) * 128)
+            gi_fin[j, :, columns] = gi.total(gi_own[j, :, columns], j, e)
         for k in range(4):
+            send(gi_fin.at[j, pl.ds(k * 128, 128), :], gi_piece(j, q), gi_fin_send, gi_fin_recv, partner(k))
+
+    def gw_final(j):
+        gw_fin_own[...] = gw_own(j)
+        for e in range(2):
+            columns = slice(e * 128, (e + 1) * 128)
+            gw_fin[j, :, columns] = gw.total(gw_fin_own[:, columns], j, e)
             send(
-                gi_fin.at[j, pl.ds(k * 128, 128), :], gi_piece(j, q), gi_fin_send, gi_fin_recv,
-                partner(k),
-            )
-
-    def gw_final(j):
-        gw.total_wait(j)
-        gw_fin[j] = gw.total(gw_own[j], j)
-        for e in range(2):
-            send(
-                gw_fin.at[j, :, pl.ds(e * 128, 128)], gw_piece(j // 2, q), gw_fin_send,
-                gw_fin_recv, partner(2 * (j % 2) + e),
+                gw_fin.at[j, :, pl.ds(e * 128, 128)], gw_piece(j // 2, q), gw_fin_send, gw_fin_recv,
+                partner(2 * (j % 2) + e),
             )
 
     def steps_of(count, work, after, name):
@@ -406,60 +405,92 @@
     def forward_4():
         g_first(4)
         g_own(6)
+        g_second(3)
 
     def forward_5():
-        g_first(5)
+        g_forward(5)
         g_own(7)
-
-    steps_of(2, lambda h: gi_far_pair(2 * h), {0: forward_4, 1: lambda: g_second(3)}, "s16_gifar")
+        g_second(4)
+        g_first_to_mate(5)
+
+    steps_of(2, lambda h: gi_far_pair(2 * h), {0: forward_4}, "s16_gifar")
     with jax.named_scope("s17_gm23"):
         g_from_mate(2)
         g_from_mate(3)
-    steps_of(2, gi_near_part, {0: forward_5, 1: lambda: g_second(4)}, "s18_gipart")
+    steps_of(2, gi_near_part, {0: forward_5}, "s18_gipart")
     with jax.named_scope("s19_trest"):
         t_ring.rest()
         g_from_mate(4)
-    steps_of(2, gw_far_pair, {0: lambda: g_first(6), 1: lambda: g_second(5)}, "s20_gwfar")
-    with jax.named_scope("s21_gm5"):
+    steps_of(4, gw_far, {0: lambda: g_first(6), 2: lambda: g_second(5)}, "s20_gwfar")
+    with jax.named_scope("s22_gm5"):
         g_from_mate(5)
-    steps_of(4, gw_near_part, {1: lambda: g_first(7), 3: lambda: g_second(6)}, "s22_gwpart")
-    with jax.named_scope("s23_giown"):
-        gi_own_part()
-    with jax.named_scope("s24_g7"):
-        g_second(7)
-        g_from_mate(6)
-
-    @pl.loop(0, 5)
-    def _(j):
-        @pl.when(j < 4)
-        def _():
-            with jax.named_scope("s31_ginear"):
-                gi_near(j)
-
-        @pl.when(j == 0)
+
+    @pl.loop(0, 7)
+    def _(t):
+        @pl.when(t < 4)
+        def _():
+            with jax.named_scope("s25_giright"):
+                gi_near(t, 0)
+
+        @pl.when(t == 0)
+        def _():
+            with jax.named_scope("s26_g7"):
+                g_first(7)
+
+        @pl.when(t == 1)
+        def _():
+            with jax.named_scope("s24_gm6"):
+                g_from_mate(6)
+
+        @pl.when((t > 0) & (t < 5))
+        def _():
+            with jax.named_scope("s31_gileft"):
+                gi_near(t - 1, 1)
+
+        @pl.when(t == 1)
+        def _():
+            with jax.named_scope("s28_gs7"):
+                g_second(7)
+
+        @pl.when(t < 2)
+        def _():
+            @pl.loop(0, 2)
+            def _(k):
+                with jax.named_scope("s23_gwpart"):
+                    gw_near_part(2 * t + k)
+
+        @pl.when(t == 0)
+        def _():
+            with jax.named_scope("s27_gs6"):
+                g_second(6)
+
+        @pl.when(t > 2)
+        def _():
+            with jax.named_scope("s35_gifinal"):
+                gi_final(t - 3)
+
+        @pl.when(t == 1)
         def _():
             with jax.named_scope("s30_gm7"):
                 g_from_mate(7)
 
-        @pl.when(j < 4)
+        @pl.when((t > 0) & (t < 5))
         def _():
             with jax.named_scope("s33_gwnear"):
-                gw_near(j)
-
-        @pl.when(j == 1)
-        def _():
-            with jax.named_scope("s34_gwown"):
-                gw_own_all()
-
-        @pl.when(j > 0)
-        def _():
-            with jax.named_scope("s35_gifinal"):
-                gi_final(j - 1)
+                gw_near(t - 1)
+
+        @pl.when(t == 2)
+        def _():
+            with jax.named_scope("s34_own"):
+                gi_own_all()
+
+        @pl.when(t > 2)
+        def _():
             with jax.named_scope("s36_gwfinal"):
-                gw_final(j - 1)
+                gw_final(t - 3)
 
     with jax.named_scope("s50_drain"):
-        for src, sem in ((w_hbm, w_ex_send), (tt_loc, t_ex_send), (gi_fin, gi_fin_send), (gw_fin, gw_fin_send)):
+        for src, sem in ((w_loc, w_ex_send), (tt_loc, t_ex_send), (gi_fin, gi_fin_send), (gw_fin, gw_fin_send)):
             sent_from(src, sem)
         sent_from(g.at[0:B, :], g_ring_send)
         sent_from(g.at[0:B, 0:1024], g_fw_send)
@@ -474,26 +505,38 @@
         arrived(gw_all, gw_fin_recv)
 
 
+def put(gi_from, gw_from, gi_out, gw_out, gi_sem, gw_sem):
+    copies = []
+    for k in range(4):
+        columns, rows = pl.ds(k * 1024, 1024), pl.ds(k * 1024, 1024)
+        copies.append(pltpu.make_async_copy(gi_from.at[:, columns], gi_out.at[:, columns], gi_sem.at[k]))
+        copies.append(pltpu.make_async_copy(gw_from.at[rows, :], gw_out.at[rows, :], gw_sem.at[k]))
+    for copy in copies:
+        copy.start()
+    for copy in copies:
+        copy.wait()
+
+
 def per_device(tokens, weight, grad_output):
     dma = pltpu.SemaphoreType.DMA
     codes = lambda *lead: pltpu.VMEM((*lead, CODE_ROWS, TILE), BF16)
     any_spec = pl.BlockSpec(memory_space=pl.ANY)
-    return pl.pallas_call(
+    blocks = pl.pallas_call(
         kernel,
         out_shape=(pltpu.VMEM((128, 4096), BF16), pltpu.VMEM((4096, 128), BF16)),
         in_specs=[any_spec] * 3,
         out_specs=(any_spec, any_spec),
         scratch_shapes=[
-            pltpu.VMEM((128, 4096), BF16), pltpu.VMEM((4096, 128), BF16),
+            pltpu.VMEM((128, 4096), BF16), pltpu.VMEM((4096, 128), BF16), pltpu.VMEM((4096, 128), BF16),
             pltpu.VMEM((1024, 2048), BF16), pltpu.VMEM((1024, 2048), BF16), pltpu.VMEM((2048, 2048), BF16),
             codes(4), codes(4), codes(2, 4), codes(2, 4), codes(4), codes(4), codes(2, 4), codes(2, 4),
-            pltpu.VMEM((4, B, TILE), BF16), pltpu.VMEM((4, B, TILE), BF16), pltpu.VMEM((4, B, TILE), F32),
+            pltpu.VMEM((4, B, TILE), BF16), pltpu.VMEM((4, B, TILE), BF16), pltpu.VMEM((B, TILE), F32),
             pltpu.VMEM((4, B, TILE), F32), pltpu.VMEM((2, 4, B, TILE), F32), pltpu.VMEM((4, B, 2 * TILE), F32),
-            dma(()), dma(()),
+            dma(()), dma(()), dma(()),
             dma(()), dma(()), dma((PARTS, 2)), dma((PARTS, 2)),
             dma(()), dma(()), dma(()), dma(()), dma((PARTS, 2)), dma((PARTS, 2)), dma((2,)), dma((2,)),
             dma(()), dma(()), dma(()), dma((8, 3)), dma((8,)),
-            dma(()), dma((2, 4)), dma(()), dma((2, 4)), dma(()), dma((2, 4)), dma(()), dma((2, 4)),
+            dma(()), dma((2, 4)), dma(()), dma((2, 4, 2)), dma(()), dma((2, 4)), dma(()), dma((2, 4, 2)),
             dma(()), dma(()), dma(()), dma(()),
         ],
         compiler_params=pltpu.CompilerParams(
@@ -501,6 +544,14 @@
         ),
         name="linear_backward",
     )(tokens, weight, grad_output)
+    return pl.pallas_call(
+        put,
+        out_shape=tuple(jax.ShapeDtypeStruct(block.shape, BF16) for block in blocks),
+        in_specs=[pl.BlockSpec(memory_space=pltpu.VMEM)] * 2,
+        out_specs=(any_spec, any_spec),
+        scratch_shapes=[dma((4,)), dma((4,))],
+        name="put",
+    )(*[pltpu.with_memory_space_constraint(block, pltpu.VMEM) for block in blocks])
 
 
 def solution(mesh):

time: 108 us -> 105 us (0.972)
  local copies, waits for them, and re-layouts: 1.94 us -> 0 us
    pallas_call x1, Pallas kernels: 105 us -> 103 us  [per_device(): pl.pallas_call(kernel, out_shape=(pltpu.VMEM((128, 4096), BF16), pltpu.VM...]
    unnamed x2 -> x0, local copies, waits for them, and re-layouts: 1.94 us -> none
    pallas_call x0 -> x1, Pallas kernels: none -> 1.38 us  [per_device(): pl.pallas_call(put, out_shape=tuple((jax.ShapeDtypeStruct(block.shape, BF...]
where the time goes in v3:
time: 105 us
  Pallas kernels  104 us (99%)
    pallas_call x1, Pallas kernels, per_device(): pl.pallas_call(kernel, out_shape=(pltpu.VMEM((128, 4096), BF16), pltpu.VM...  103 us

profile of v3, /device:TPU:1, one launch (start us, length us, event | category | flops | bytes accessed | tf_op | source)
XLA Modules:
  0.0 104.7 jit_solution(6365520128853646933)
XLA Ops:
  0.6 102.7 %linear_backward.1 = (bf16[128,4096]{1,0:T(8,128)(2,1)S(1)}, bf16[4096,128]{1,0:T(8,128)(2,1)S(1)}) custom-call(bf16[128,4096]{1,0:T(8,128)(2,1)} %t_hbm.1, bf16[4096,128]{1,0:T(8,128)(2,1)} %w_hbm.1, bf16[2048,256]{1,0:T(8,128)(2,1)} %g_hbm.1), custom_call_target="tpu_custom_call" | custom-call | tf_op jit(solution)/shard_map/linear_backward/pallas_call | solution.py:524
  103.3 1.4 %put.1 = (bf16[128,4096]{1,0:T(8,128)(2,1)}, bf16[4096,128]{1,0:T(8,128)(2,1)}) custom-call(bf16[128,4096]{1,0:T(8,128)(2,1)S(1)} %get-tuple-element.4.gi_from, bf16[4096,128]{1,0:T(8,128)(2,1)S(1)} %get-tuple-element.5.gw_from), custom_call_target="tpu_custom_call" | custom-call | tf_op jit(solution)/shard_map/put/pallas_call | solution.py:547

commit v4 on v3

--- a/solution.py
+++ b/solution.py
@@ -38,17 +38,17 @@
     ref[B:CODE_ROWS, :] = jnp.broadcast_to(scale.astype(F32), (8, tile.shape[1])).astype(BF16)
 
 
-def decode(ref):
-    code = ref[0:B, :].astype(F32)
+def decode(ref, first=0, rows=B):
+    code = ref[first : first + rows, :].astype(F32)
     scale = ref[B:CODE_ROWS, :].astype(F32)[0:1] * (1.0 / TOP)
     size = jnp.exp2(jnp.log2(jnp.abs(code)) * (1.0 / POWER))
     return jnp.where(code < 0, -size, size) * scale
 
 
 class Reduction:
-    def __init__(self, send, arrived, at, far_tx, hop, tx, rx, far_send, hop_recv, send_sem, recv):
+    def __init__(self, send, arrived, at, far_tx, hop, tx, rx, far_send, hop_recv, send_sem, recv, parts):
         self.send, self.arrived, self.at, self.far_tx, self.hop, self.tx, self.rx = send, arrived, at, far_tx, hop, tx, rx
-        self.far_send, self.hop_recv, self.send_sem, self.recv = far_send, hop_recv, send_sem, recv
+        self.far_send, self.hop_recv, self.send_sem, self.recv, self.parts = far_send, hop_recv, send_sem, recv, parts
 
     def half(self, ref, j, side):
         return ref.at[j, :, pl.ds(side * 128, 128)]
@@ -72,16 +72,16 @@
         encode(jnp.concatenate(parts, axis=1), self.tx.at[side, j])
 
     def near_start(self, j, side):
-        for e in range(2):
+        for part, rows in enumerate(self.parts):
             self.send(
-                self.half(self.tx.at[side], j, e), self.half(self.rx.at[side], j, e), self.send_sem,
-                self.recv.at[side, j, e], self.at(1 + 2 * side),
+                self.tx.at[side, j, rows], self.rx.at[side, j, rows], self.send_sem, self.recv.at[side, j, part],
+                self.at(1 + 2 * side),
             )
 
-    def total(self, own, j, e):
+    def total(self, own, j, part, first, rows):
         for side in range(2):
-            self.arrived(self.half(self.rx.at[side], j, e), self.recv.at[side, j, e])
-        return (own + decode(self.half(self.rx.at[0], j, e)) + decode(self.half(self.rx.at[1], j, e))).astype(BF16)
+            self.arrived(self.rx.at[side, j, self.parts[part]], self.recv.at[side, j, part])
+        return (own + decode(self.rx.at[0, j], first, rows) + decode(self.rx.at[1, j], first, rows)).astype(BF16)
 
     def drain(self, sent_from):
         sent_from(self.far_tx, self.far_send)
@@ -138,7 +138,7 @@
     def g_lane(owner, owner_core, late):
         member = (2 * (owner % 2) + (z + late) % 2 - z + 4) % 4
         second = (1 - member // 2) if late == 0 else member // 2
-        return pl.multiple_of(late * 1024 + (owner // 2) * 512 + second * 256 + owner_core * 128, 128)
+        return pl.multiple_of(late * 1024 + owner_core * 512 + second * 256 + (owner // 2) * 128, 128)
 
     def g_piece(s, dy, other_core=False, half=None):
         member, late = steps[s]
@@ -167,22 +167,22 @@
     def part_rows(part):
         return pl.ds(part * PART, PART)
 
-    def exchange(src, ref, lane, ex_send, ex_recv, part):
+    def exchange(src, ref, lane, pair, ex_send, ex_recv, part):
         for k in range(4):
             piece = src.at[pl.ds(k * 1024 + part * PART, PART), :]
-            send(piece, ref.at[part_rows(part), pl.ds(lane, 128)], ex_send, ex_recv.at[part, q // 2], partner(k))
-
-    w_own_lane = pl.multiple_of((q // 2) * 512 + 256 + (q % 2) * 128, 128)
+            send(piece, ref.at[part_rows(part), pl.ds(lane, 128)], ex_send, ex_recv.at[part, pair], partner(k))
+
+    w_own_lane = pl.multiple_of(core * 512 + 256 + yh * 128, 128)
     t_own_lane = pl.multiple_of(TOKEN_SLOT[OWN] * B + q * 128, 128)
     w_copy.wait()
-    exchange(w_loc, w, w_own_lane, w_ex_send, w_ex_recv, 0)
+    exchange(w_loc, w, w_own_lane, core, w_ex_send, w_ex_recv, 0)
     t_copy.wait()
     for k in range(8):
         tt_loc[k * 512 : k * 512 + 512, :] = t_loc[:, k * 512 : k * 512 + 512].T
-    exchange(tt_loc, tt, t_own_lane, t_ex_send, t_ex_recv, 0)
+    exchange(tt_loc, tt, t_own_lane, yh, t_ex_send, t_ex_recv, 0)
     for part in range(1, PARTS):
-        exchange(w_loc, w, w_own_lane, w_ex_send, w_ex_recv, part)
-        exchange(tt_loc, tt, t_own_lane, t_ex_send, t_ex_recv, part)
+        exchange(w_loc, w, w_own_lane, core, w_ex_send, w_ex_recv, part)
+        exchange(tt_loc, tt, t_own_lane, yh, t_ex_send, t_ex_recv, part)
 
     def g_own(s):
         piece = g_piece(s, 0)
@@ -314,8 +314,9 @@
         columns = pl.ds(pl.multiple_of(lane + (j % 2) * 512, 512), 512)
         return jnp.dot(tt[rows, first : first + terms], g[first : first + terms, columns], preferred_element_type=F32)
 
-    gi = Reduction(send, arrived, at_x, gi_far_tx, gi_hop, gi_tx, gi_rx, gi_far_send, gi_hop_recv, gi_send, gi_recv)
-    gw = Reduction(send, arrived, at_z, gw_far_tx, gw_hop, gw_tx, gw_rx, gw_far_send, gw_hop_recv, gw_send, gw_recv)
+    whole, in_two = (pl.ds(0, CODE_ROWS),), (pl.ds(B // 2, CODE_ROWS - B // 2), pl.ds(0, B // 2))
+    gi = Reduction(send, arrived, at_x, gi_far_tx, gi_hop, gi_tx, gi_rx, gi_far_send, gi_hop_recv, gi_send, gi_recv, whole)
+    gw = Reduction(send, arrived, at_z, gw_far_tx, gw_hop, gw_tx, gw_rx, gw_far_send, gw_hop_recv, gw_send, gw_recv, in_two)
 
     def gi_far_pair(j):
         both = gi_dot(0, 1, j, 2)
@@ -342,12 +343,13 @@
             for k in range(2):
                 gi_part[side, 2 * h + k] = both[side * B : (side + 1) * B, k * TILE : (k + 1) * TILE]
 
-    def gi_own_all():
+    def gi_own_terms(first):
         @pl.loop(0, 2)
         def _(h):
-            both = gi_dot(3, 1, 2 * h, 2)
+            both = gi_dot(3, 1, 2 * h, 2, first, HALF)
             for k in range(2):
-                gi_own[2 * h + k] = both[:, k * TILE : (k + 1) * TILE]
+                terms = both[:, k * TILE : (k + 1) * TILE]
+                gi_own[2 * h + k] = terms if first == 0 else gi_own[2 * h + k] + terms
 
     def gw_near_part(j):
         gw_part[j] = gw_dot(1024, j, 0, HALF)
@@ -370,25 +372,24 @@
     def gi_piece(j, k):
         return gi_all.at[:, pl.ds(pl.multiple_of(k * 1024 + j * TILE, TILE), TILE)]
 
-    def gw_piece(i, k):
-        return gw_all.at[pl.ds(pl.multiple_of(k * 1024 + i * B, B), B), :]
+    def gw_piece(i, first):
+        return gw_all.at[pl.ds(pl.multiple_of(q * 1024 + i * B + first, B // 2), B // 2), :]
 
     def gi_final(j):
-        for e in range(2):
-            columns = slice(e * 128, (e + 1) * 128)
-            gi_fin[j, :, columns] = gi.total(gi_own[j, :, columns], j, e)
+        gi_fin[j] = gi.total(gi_own[j], j, 0, 0, B)
         for k in range(4):
             send(gi_fin.at[j, pl.ds(k * 128, 128), :], gi_piece(j, q), gi_fin_send, gi_fin_recv, partner(k))
 
     def gw_final(j):
         gw_fin_own[...] = gw_own(j)
-        for e in range(2):
-            columns = slice(e * 128, (e + 1) * 128)
-            gw_fin[j, :, columns] = gw.total(gw_fin_own[:, columns], j, e)
-            send(
-                gw_fin.at[j, :, pl.ds(e * 128, 128)], gw_piece(j // 2, q), gw_fin_send, gw_fin_recv,
-                partner(2 * (j % 2) + e),
-            )
+        for part, first in enumerate((B // 2, 0)):
+            rows = slice(first, first + B // 2)
+            gw_fin[j, rows, :] = gw.total(gw_fin_own[rows, :], j, part, first, B // 2)
+            for e in range(2):
+                send(
+                    gw_fin.at[j, pl.ds(first, B // 2), pl.ds(e * 128, 128)], gw_piece(j // 2, first), gw_fin_send,
+                    gw_fin_recv, partner(j % 2 + 2 * e),
+                )
 
     def steps_of(count, work, after, name):
         @pl.loop(0, count)
@@ -425,69 +426,68 @@
     with jax.named_scope("s22_gm5"):
         g_from_mate(5)
 
-    @pl.loop(0, 7)
-    def _(t):
-        @pl.when(t < 4)
-        def _():
-            with jax.named_scope("s25_giright"):
-                gi_near(t, 0)
-
-        @pl.when(t == 0)
-        def _():
-            with jax.named_scope("s26_g7"):
-                g_first(7)
-
-        @pl.when(t == 1)
-        def _():
-            with jax.named_scope("s24_gm6"):
-                g_from_mate(6)
-
-        @pl.when((t > 0) & (t < 5))
+    with jax.named_scope("s25_giright0"):
+        gi_near(0, 0)
+    with jax.named_scope("s26_g7"):
+        g_first(7)
+
+    @pl.loop(0, 2)
+    def _(j):
+        with jax.named_scope("s27_gwpart"):
+            gw_near_part(j)
+
+    with jax.named_scope("s28_gs6"):
+        g_second(6)
+    with jax.named_scope("s29_giright1"):
+        gi_near(1, 0)
+    with jax.named_scope("s30_gm6"):
+        g_from_mate(6)
+
+    @pl.loop(0, 5)
+    def _(u):
+        @pl.when(u < 4)
         def _():
             with jax.named_scope("s31_gileft"):
-                gi_near(t - 1, 1)
-
-        @pl.when(t == 1)
-        def _():
-            with jax.named_scope("s28_gs7"):
+                gi_near(u, 1)
+
+        @pl.when(u == 0)
+        def _():
+            with jax.named_scope("s32_gs7"):
                 g_second(7)
 
-        @pl.when(t < 2)
-        def _():
-            @pl.loop(0, 2)
-            def _(k):
-                with jax.named_scope("s23_gwpart"):
-                    gw_near_part(2 * t + k)
-
-        @pl.when(t == 0)
-        def _():
-            with jax.named_scope("s27_gs6"):
-                g_second(6)
-
-        @pl.when(t > 2)
-        def _():
-            with jax.named_scope("s35_gifinal"):
-                gi_final(t - 3)
-
-        @pl.when(t == 1)
-        def _():
-            with jax.named_scope("s30_gm7"):
+        for at in range(2):
+
+            @pl.when(u == at)
+            def _():
+                with jax.named_scope("s33_giown"):
+                    gi_own_terms(at * HALF)
+
+        @pl.when(u == 0)
+        def _():
+            with jax.named_scope("s34_gm7"):
                 g_from_mate(7)
 
-        @pl.when((t > 0) & (t < 5))
-        def _():
-            with jax.named_scope("s33_gwnear"):
-                gw_near(t - 1)
-
-        @pl.when(t == 2)
-        def _():
-            with jax.named_scope("s34_own"):
-                gi_own_all()
-
-        @pl.when(t > 2)
-        def _():
-            with jax.named_scope("s36_gwfinal"):
-                gw_final(t - 3)
+        @pl.when(u < 4)
+        def _():
+            with jax.named_scope("s35_gwnear"):
+                gw_near(u)
+
+        @pl.when(u > 0)
+        def _():
+            with jax.named_scope("s36_gifinal"):
+                gi_final(u - 1)
+
+        @pl.when(u < 2)
+        def _():
+            with jax.named_scope("s37_giright"):
+                gi_near(u + 2, 0)
+            with jax.named_scope("s38_gwpart"):
+                gw_near_part(u + 2)
+
+        @pl.when(u > 0)
+        def _():
+            with jax.named_scope("s39_gwfinal"):
+                gw_final(u - 1)
 
     with jax.named_scope("s50_drain"):
         for src, sem in ((w_loc, w_ex_send), (tt_loc, t_ex_send), (gi_fin, gi_fin_send), (gw_fin, gw_fin_send)):
@@ -536,7 +536,7 @@
             dma(()), dma(()), dma((PARTS, 2)), dma((PARTS, 2)),
             dma(()), dma(()), dma(()), dma(()), dma((PARTS, 2)), dma((PARTS, 2)), dma((2,)), dma((2,)),
             dma(()), dma(()), dma(()), dma((8, 3)), dma((8,)),
-            dma(()), dma((2, 4)), dma(()), dma((2, 4, 2)), dma(()), dma((2, 4)), dma(()), dma((2, 4, 2)),
+            dma(()), dma((2, 4)), dma(()), dma((2, 4, 1)), dma(()), dma((2, 4)), dma(()), dma((2, 4, 2)),
             dma(()), dma(()), dma(()), dma(()),
         ],
         compiler_params=pltpu.CompilerParams(

time: 105 us -> 104 us (level)
    pallas_call x1, Pallas kernels: 103 us -> 101 us  [per_device(): pl.pallas_call(kernel, out_shape=(pltpu.VMEM((128, 4096), BF16), pltpu.VM...]
where the time goes in v4:
time: 104 us; the launch traced here: 103 us
  Pallas kernels  103 us (99%)
    pallas_call x1, Pallas kernels, per_device(): pl.pallas_call(kernel, out_shape=(pltpu.VMEM((128, 4096), BF16), pltpu.VM...  101 us

profile of v4, /device:TPU:1, one launch (start us, length us, event | category | flops | bytes accessed | tf_op | source)
XLA Modules:
  0.0 103.4 jit_solution(18247381232587748238)
XLA Ops:
  0.6 101.4 %linear_backward.1 = (bf16[128,4096]{1,0:T(8,128)(2,1)S(1)}, bf16[4096,128]{1,0:T(8,128)(2,1)S(1)}) custom-call(bf16[128,4096]{1,0:T(8,128)(2,1)} %t_hbm.1, bf16[4096,128]{1,0:T(8,128)(2,1)} %w_hbm.1, bf16[2048,256]{1,0:T(8,128)(2,1)} %g_hbm.1), custom_call_target="tpu_custom_call" | custom-call | tf_op jit(solution)/shard_map/linear_backward/pallas_call | solution.py:524
  102.0 1.4 %put.1 = (bf16[128,4096]{1,0:T(8,128)(2,1)}, bf16[4096,128]{1,0:T(8,128)(2,1)}) custom-call(bf16[128,4096]{1,0:T(8,128)(2,1)S(1)} %get-tuple-element.4.gi_from, bf16[4096,128]{1,0:T(8,128)(2,1)S(1)} %get-tuple-element.5.gw_from), custom_call_target="tpu_custom_call" | custom-call | tf_op jit(solution)/shard_map/put/pallas_call | solution.py:547

commit v5 on v4

--- a/solution.py
+++ b/solution.py
@@ -74,13 +74,12 @@
     def near_start(self, j, side):
         for part, rows in enumerate(self.parts):
             self.send(
-                self.tx.at[side, j, rows], self.rx.at[side, j, rows], self.send_sem, self.recv.at[side, j, part],
+                self.tx.at[side, j, rows], self.rx.at[side, j, rows], self.send_sem, self.recv.at[j, part],
                 self.at(1 + 2 * side),
             )
 
     def total(self, own, j, part, first, rows):
-        for side in range(2):
-            self.arrived(self.rx.at[side, j, self.parts[part]], self.recv.at[side, j, part])
+        self.arrived(self.rx.at[:, j, self.parts[part]], self.recv.at[j, part])
         return (own + decode(self.rx.at[0, j], first, rows) + decode(self.rx.at[1, j], first, rows)).astype(BF16)
 
     def drain(self, sent_from):
@@ -167,22 +166,22 @@
     def part_rows(part):
         return pl.ds(part * PART, PART)
 
-    def exchange(src, ref, lane, pair, ex_send, ex_recv, part):
+    def exchange(src, ref, lane, ex_send, ex_recv, part):
         for k in range(4):
             piece = src.at[pl.ds(k * 1024 + part * PART, PART), :]
-            send(piece, ref.at[part_rows(part), pl.ds(lane, 128)], ex_send, ex_recv.at[part, pair], partner(k))
+            send(piece, ref.at[part_rows(part), pl.ds(lane, 128)], ex_send, ex_recv.at[part], partner(k))
 
     w_own_lane = pl.multiple_of(core * 512 + 256 + yh * 128, 128)
     t_own_lane = pl.multiple_of(TOKEN_SLOT[OWN] * B + q * 128, 128)
     w_copy.wait()
-    exchange(w_loc, w, w_own_lane, core, w_ex_send, w_ex_recv, 0)
+    exchange(w_loc, w, w_own_lane, w_ex_send, w_ex_recv, 0)
     t_copy.wait()
     for k in range(8):
         tt_loc[k * 512 : k * 512 + 512, :] = t_loc[:, k * 512 : k * 512 + 512].T
-    exchange(tt_loc, tt, t_own_lane, yh, t_ex_send, t_ex_recv, 0)
+    exchange(tt_loc, tt, t_own_lane, t_ex_send, t_ex_recv, 0)
     for part in range(1, PARTS):
-        exchange(w_loc, w, w_own_lane, core, w_ex_send, w_ex_recv, part)
-        exchange(tt_loc, tt, t_own_lane, yh, t_ex_send, t_ex_recv, part)
+        exchange(w_loc, w, w_own_lane, w_ex_send, w_ex_recv, part)
+        exchange(tt_loc, tt, t_own_lane, t_ex_send, t_ex_recv, part)
 
     def g_own(s):
         piece = g_piece(s, 0)
@@ -229,9 +228,9 @@
             return self.ref.at[part_rows(part), pl.ds(self.lane(member, pair), 256)]
 
         def own(self, part):
+            arrived(self.ref.at[part_rows(part), 0:512], self.ex_recv.at[part])
             for pair in range(2):
                 piece = self.piece(OWN, part, pair)
-                arrived(piece, self.ex_recv.at[part, pair])
                 for side, member in ((0, LEFT), (1, RIGHT)):
                     kept = (part < PARTS // 2) == (side == 1)
                     sem = self.rest_recv.at[0] if kept else self.recv.at[part, pair]
@@ -533,10 +532,10 @@
             pltpu.VMEM((4, B, TILE), BF16), pltpu.VMEM((4, B, TILE), BF16), pltpu.VMEM((B, TILE), F32),
             pltpu.VMEM((4, B, TILE), F32), pltpu.VMEM((2, 4, B, TILE), F32), pltpu.VMEM((4, B, 2 * TILE), F32),
             dma(()), dma(()), dma(()),
-            dma(()), dma(()), dma((PARTS, 2)), dma((PARTS, 2)),
+            dma(()), dma(()), dma((PARTS,)), dma((PARTS,)),
             dma(()), dma(()), dma(()), dma(()), dma((PARTS, 2)), dma((PARTS, 2)), dma((2,)), dma((2,)),
             dma(()), dma(()), dma(()), dma((8, 3)), dma((8,)),
-            dma(()), dma((2, 4)), dma(()), dma((2, 4, 1)), dma(()), dma((2, 4)), dma(()), dma((2, 4, 2)),
+            dma(()), dma((2, 4)), dma(()), dma((4, 1)), dma(()), dma((2, 4)), dma(()), dma((4, 2)),
             dma(()), dma(()), dma(()), dma(()),
         ],
         compiler_params=pltpu.CompilerParams(

time: 104 us -> 103 us (level)
  no operation moved by 1% of the time
where the time goes in v5:
time: 103 us
  Pallas kernels  103 us (100%)
    pallas_call x1, Pallas kernels, per_device(): pl.pallas_call(kernel, out_shape=(pltpu.VMEM((128, 4096), BF16), pltpu.VM...  101 us

profile of v5, /device:TPU:1, one launch (start us, length us, event | category | flops | bytes accessed | tf_op | source)
XLA Modules:
  0.0 103.2 jit_solution(7367874869335548722)
XLA Ops:
  0.6 101.2 %linear_backward.1 = (bf16[128,4096]{1,0:T(8,128)(2,1)S(1)}, bf16[4096,128]{1,0:T(8,128)(2,1)S(1)}) custom-call(bf16[128,4096]{1,0:T(8,128)(2,1)} %t_hbm.1, bf16[4096,128]{1,0:T(8,128)(2,1)} %w_hbm.1, bf16[2048,256]{1,0:T(8,128)(2,1)} %g_hbm.1), custom_call_target="tpu_custom_call" | custom-call | tf_op jit(solution)/shard_map/linear_backward/pallas_call | solution.py:523
  101.8 1.4 %put.1 = (bf16[128,4096]{1,0:T(8,128)(2,1)}, bf16[4096,128]{1,0:T(8,128)(2,1)}) custom-call(bf16[128,4096]{1,0:T(8,128)(2,1)S(1)} %get-tuple-element.4.gi_from, bf16[4096,128]{1,0:T(8,128)(2,1)S(1)} %get-tuple-element.5.gw_from), custom_call_target="tpu_custom_call" | custom-call | tf_op jit(solution)/shard_map/put/pallas_call | solution.py:546
